TPU v7x, 32 devices: a whole 2x2x4 slice. The times are simulated.
32 devices in a mesh: row: 8 (over z, x), col: 4 (over y, core).
Axes of the slice: x: 2, y: 2, z: 4, core: 2. Of those that a mesh axis runs over, the one named last changes fastest.
Arguments:
- eigvecs: float32 [2048, 512], P('row', 'col'), may hold values from -6 to 6
- reflectors: float32 [8, 32, 128, 64], P(None, ('row', 'col')), may hold values from -2 to 2, as said below
- factors: float32 [8, 32, 64, 64], P(None, ('row', 'col')), may hold values from -3 to 3, as said below
- order: int32 [8], replicated, may hold values from 0 to 7, each once
- offsets: int32 [8], replicated, may hold values from 0 to 63
Outputs:
- rotated: float32 [2048, 512], P('row', 'col')
Inputs may be any that keep to these rules, and one draw needn't show every extreme that they name: `order`: a permutation of 0 .. 7. Every block map is orthogonal: with V the block of reflectors and T the block of factors, T is upper triangular and T^-1 + T^-T = V^T V. `factors`: upper triangular, paired with reflectors as promised there.
All inputs are finite; a program needn't handle non-finite values.
Results may differ from a plain program's by a relative error of at most 0.0003.
Values sent between devices are 32-bit elements; how exact they have to be, the bound alone decides.
A program may use at most 64 MiB of HBM per device.

v0:
```python
import jax
import jax.numpy as jnp
from jax import lax
from jax.sharding import PartitionSpec as P

highest = lax.Precision.HIGHEST


def passed_along(block, axis, distance):
    devices = range(lax.axis_size(axis))
    route = [(i - distance, i) for i in devices if i - distance in devices]
    return lax.ppermute(block, axis, route)


def entering(array, axis, combine, identity):
    size, position = (lax.axis_size(axis), lax.axis_index(axis))
    everything = jax.tree.map(lambda part: lax.all_gather(part, axis), array)
    start = jax.tree.map(
        lambda part, zero: jnp.broadcast_to(jnp.asarray(zero, part.dtype), part.shape),
        array,
        identity,
    )

    def hop(k, before):
        reached = k < position
        new = combine(before, jax.tree.map(lambda part: part[k], everything))
        return jax.tree.map(lambda a, b: jnp.where(reached, a, b), new, before)

    return lax.fori_loop(0, size, hop, start)


def reflect(segment, householder, triangle):
    inner = jnp.dot(householder.T, segment, precision=highest, preferred_element_type=jnp.float32)
    inner = jnp.dot(triangle, inner, precision=highest, preferred_element_type=jnp.float32)
    return segment - jnp.dot(
        householder, inner, precision=highest, preferred_element_type=jnp.float32
    )


def sweep_apply(extended, house_set, tri_set, offset):
    block_width = house_set.shape[-1]

    def advance(number, current):
        start = offset + number * block_width
        segment = lax.dynamic_slice_in_dim(current, start, 2 * block_width, 0)
        householder = lax.dynamic_index_in_dim(house_set, number, 0, keepdims=False)
        triangle = lax.dynamic_index_in_dim(tri_set, number, 0, keepdims=False)
        return lax.dynamic_update_slice_in_dim(
            current, reflect(segment, householder, triangle), start, 0
        )

    return lax.fori_loop(0, house_set.shape[0], advance, extended)


def compose(earlier, later):
    first_map = jnp.dot(later[0], earlier[0], precision=highest, preferred_element_type=jnp.float32)
    shifted = (
        jnp.dot(later[0], earlier[1], precision=highest, preferred_element_type=jnp.float32)
        + later[1]
    )
    return (first_map, shifted)


def local(eigvecs, reflectors, factors, order, offsets):
    height = eigvecs.shape[0]
    columns = eigvecs.shape[1]
    block_width = reflectors.shape[-1]
    span_rows = 2 * block_width
    leading = lax.axis_index("row") == 0
    identity = jnp.eye(span_rows, dtype=jnp.float32)
    probe = jnp.concatenate([identity, jnp.zeros((height, span_rows), jnp.float32)], 0)
    vectors = eigvecs
    for position in range(order.shape[0]):
        stored = order[position]
        offset = offsets[stored]
        own_house = lax.dynamic_index_in_dim(reflectors, stored, 0, keepdims=False)
        own_tri = lax.dynamic_index_in_dim(factors, stored, 0, keepdims=False)
        house_set, tri_set = (
            lax.all_gather(own_house, "col", axis=0, tiled=True),
            lax.all_gather(own_tri, "col", axis=0, tiled=True),
        )
        next_rows = passed_along(vectors[:span_rows], "row", -1)
        top_rows = jnp.where(leading, vectors[:span_rows], 0.0)
        extended = jnp.concatenate([top_rows, vectors[span_rows:], next_rows], 0)
        joined = sweep_apply(jnp.concatenate([extended, probe], 1), house_set, tri_set, offset)
        partial_value = joined[:, :columns]
        response = joined[:, columns:]
        transfer = jnp.where(leading, 0.0, response[height:])
        empty = jnp.zeros((span_rows, columns), jnp.float32)
        composed = entering((transfer, partial_value[height:]), "row", compose, (identity, empty))
        incoming = composed[1]
        vectors = partial_value[:height] + jnp.dot(
            response[:height], incoming, precision=highest, preferred_element_type=jnp.float32
        )
    return vectors


def solution(mesh):
    placed = (
        P("row", "col"),
        P(None, ("row", "col"), None, None),
        P(None, ("row", "col"), None, None),
        P(),
        P(),
    )
    return jax.shard_map(
        local, mesh=mesh, in_specs=placed, out_specs=P("row", "col"), check_vma=False
    )
```

profile of v0, /device:TPU:0, one launch (start us, length us, event | category | flops | bytes accessed | tf_op | source)
XLA Modules:
  0.0 719.6 jit_solution(1707958535803900348)
XLA Ops:
  33.2 9.2 %while.216 = (s32[]{:T(128)}, f32[384,256]{1,0:T(8,128)S(1)}, s32[]{:T(128)}, f32[4,128,64]{1,2,0:T(8,128)S(1)}, f32[4,64,64]{2,1,0:T(8,128)S(1)}, /*index=5*/s32[]{:T(128)}, s32[]{:T(128)}, s32[]{:T(128)}, s32[]{:T(128)}) while((s32[]{:T(128)}, f32[384,256]{1,0:T(8,128)S(1)}, s32[]{:T(128)}, f32[4,128,64]{1,2,0:T(8,128)S(1)}, ...), condition=%wide.region_1.2_spmd, body=%wide.region_0.1_spmd.sunk | while | flops 62947336 | bytes 1015983 | solution.py:52
  42.5 34.1 %all-gather.2 = f32[1024,128]{1,0:T(8,128)S(1)} all-gather(f32[128,128]{1,0:T(8,128)S(1)} %get-tuple-element.1884), channel_id=4, replica_groups=mesh['row'=8,'col'=4] {'row'}, dimensions={0}, use_global_device_ids=true | all-gather | bytes 589824 | tf_op jit(solution)/shard_map/all_gather | solution.py:17
  76.6 31.2 %all-gather.3 = f32[1024,128]{1,0:T(8,128)S(1)} all-gather(f32[128,128]{1,0:T(8,128)S(1)} %get-tuple-element.1883), channel_id=5, replica_groups=mesh['row'=8,'col'=4] {'row'}, dimensions={0}, use_global_device_ids=true | all-gather | bytes 589824 | tf_op jit(solution)/shard_map/all_gather | solution.py:17
  122.2 9.4 %while.217 = (s32[]{:T(128)}, f32[384,256]{1,0:T(8,128)S(1)}, s32[]{:T(128)}, f32[4,128,64]{1,2,0:T(8,128)S(1)}, f32[4,64,64]{2,1,0:T(8,128)S(1)}, /*index=5*/s32[]{:T(128)}, s32[]{:T(128)}, s32[]{:T(128)}, s32[]{:T(128)}) while((s32[]{:T(128)}, f32[384,256]{1,0:T(8,128)S(1)}, s32[]{:T(128)}, f32[4,128,64]{1,2,0:T(8,128)S(1)}, ...), condition=%wide.region_5.6_spmd, body=%wide.region_4.5_spmd.sunk | while | flops 62947336 | bytes 1015983 | solution.py:52
  131.6 31.7 %all-gather.6 = f32[1024,128]{1,0:T(8,128)S(1)} all-gather(f32[128,128]{1,0:T(8,128)S(1)} %get-tuple-element.1882), channel_id=8, replica_groups=mesh['row'=8,'col'=4] {'row'}, dimensions={0}, use_global_device_ids=true | all-gather | bytes 589824 | tf_op jit(solution)/shard_map/all_gather | solution.py:17
  163.3 31.4 %all-gather.7 = f32[1024,128]{1,0:T(8,128)S(1)} all-gather(f32[128,128]{1,0:T(8,128)S(1)} %get-tuple-element.1881), channel_id=9, replica_groups=mesh['row'=8,'col'=4] {'row'}, dimensions={0}, use_global_device_ids=true | all-gather | bytes 589824 | tf_op jit(solution)/shard_map/all_gather | solution.py:17
  209.1 9.1 %while.218 = (s32[]{:T(128)}, f32[384,256]{1,0:T(8,128)S(1)}, s32[]{:T(128)}, f32[4,128,64]{1,2,0:T(8,128)S(1)}, f32[4,64,64]{2,1,0:T(8,128)S(1)}, /*index=5*/s32[]{:T(128)}, s32[]{:T(128)}, s32[]{:T(128)}, s32[]{:T(128)}) while((s32[]{:T(128)}, f32[384,256]{1,0:T(8,128)S(1)}, s32[]{:T(128)}, f32[4,128,64]{1,2,0:T(8,128)S(1)}, ...), condition=%wide.region_9.10_spmd, body=%wide.region_8.9_spmd.sunk | while | flops 62947336 | bytes 1015983 | solution.py:52
  218.2 31.8 %all-gather.10 = f32[1024,128]{1,0:T(8,128)S(1)} all-gather(f32[128,128]{1,0:T(8,128)S(1)} %get-tuple-element.1880), channel_id=12, replica_groups=mesh['row'=8,'col'=4] {'row'}, dimensions={0}, use_global_device_ids=true | all-gather | bytes 589824 | tf_op jit(solution)/shard_map/all_gather | solution.py:17
  250.0 31.5 %all-gather.11 = f32[1024,128]{1,0:T(8,128)S(1)} all-gather(f32[128,128]{1,0:T(8,128)S(1)} %get-tuple-element.1879), channel_id=13, replica_groups=mesh['row'=8,'col'=4] {'row'}, dimensions={0}, use_global_device_ids=true | all-gather | bytes 589824 | tf_op jit(solution)/shard_map/all_gather | solution.py:17
  295.9 9.5 %while.219 = (s32[]{:T(128)}, f32[384,256]{1,0:T(8,128)S(1)}, s32[]{:T(128)}, f32[4,128,64]{1,2,0:T(8,128)S(1)}, f32[4,64,64]{2,1,0:T(8,128)S(1)}, /*index=5*/s32[]{:T(128)}, s32[]{:T(128)}, s32[]{:T(128)}, s32[]{:T(128)}) while((s32[]{:T(128)}, f32[384,256]{1,0:T(8,128)S(1)}, s32[]{:T(128)}, f32[4,128,64]{1,2,0:T(8,128)S(1)}, ...), condition=%wide.region_13.14_spmd, body=%wide.region_12.13_spmd.sunk | while | flops 62947336 | bytes 1015983 | solution.py:52
  305.5 31.9 %all-gather.14 = f32[1024,128]{1,0:T(8,128)S(1)} all-gather(f32[128,128]{1,0:T(8,128)S(1)} %get-tuple-element.1878), channel_id=16, replica_groups=mesh['row'=8,'col'=4] {'row'}, dimensions={0}, use_global_device_ids=true | all-gather | bytes 589824 | tf_op jit(solution)/shard_map/all_gather | solution.py:17
  337.3 31.5 %all-gather.15 = f32[1024,128]{1,0:T(8,128)S(1)} all-gather(f32[128,128]{1,0:T(8,128)S(1)} %get-tuple-element.1877), channel_id=17, replica_groups=mesh['row'=8,'col'=4] {'row'}, dimensions={0}, use_global_device_ids=true | all-gather | bytes 589824 | tf_op jit(solution)/shard_map/all_gather | solution.py:17
  383.3 9.3 %while.220 = (s32[]{:T(128)}, f32[384,256]{1,0:T(8,128)S(1)}, s32[]{:T(128)}, f32[4,128,64]{1,2,0:T(8,128)S(1)}, f32[4,64,64]{2,1,0:T(8,128)S(1)}, /*index=5*/s32[]{:T(128)}, s32[]{:T(128)}, s32[]{:T(128)}, s32[]{:T(128)}) while((s32[]{:T(128)}, f32[384,256]{1,0:T(8,128)S(1)}, s32[]{:T(128)}, f32[4,128,64]{1,2,0:T(8,128)S(1)}, ...), condition=%wide.region_17.18_spmd, body=%wide.region_16.17_spmd.sunk | while | flops 62947336 | bytes 1015983 | solution.py:52
  392.6 31.6 %all-gather.18 = f32[1024,128]{1,0:T(8,128)S(1)} all-gather(f32[128,128]{1,0:T(8,128)S(1)} %get-tuple-element.1876), channel_id=20, replica_groups=mesh['row'=8,'col'=4] {'row'}, dimensions={0}, use_global_device_ids=true | all-gather | bytes 589824 | tf_op jit(solution)/shard_map/all_gather | solution.py:17
  424.2 31.3 %all-gather.19 = f32[1024,128]{1,0:T(8,128)S(1)} all-gather(f32[128,128]{1,0:T(8,128)S(1)} %get-tuple-element.1875), channel_id=21, replica_groups=mesh['row'=8,'col'=4] {'row'}, dimensions={0}, use_global_device_ids=true | all-gather | bytes 589824 | tf_op jit(solution)/shard_map/all_gather | solution.py:17
  470.0 9.6 %while.221 = (s32[]{:T(128)}, f32[384,256]{1,0:T(8,128)S(1)}, s32[]{:T(128)}, f32[4,128,64]{1,2,0:T(8,128)S(1)}, f32[4,64,64]{2,1,0:T(8,128)S(1)}, /*index=5*/s32[]{:T(128)}, s32[]{:T(128)}, s32[]{:T(128)}, s32[]{:T(128)}) while((s32[]{:T(128)}, f32[384,256]{1,0:T(8,128)S(1)}, s32[]{:T(128)}, f32[4,128,64]{1,2,0:T(8,128)S(1)}, ...), condition=%wide.region_21.22_spmd, body=%wide.region_20.21_spmd.sunk | while | flops 62947336 | bytes 1015983 | solution.py:52
  479.6 31.8 %all-gather.22 = f32[1024,128]{1,0:T(8,128)S(1)} all-gather(f32[128,128]{1,0:T(8,128)S(1)} %get-tuple-element.1874), channel_id=24, replica_groups=mesh['row'=8,'col'=4] {'row'}, dimensions={0}, use_global_device_ids=true | all-gather | bytes 589824 | tf_op jit(solution)/shard_map/all_gather | solution.py:17
  511.4 31.4 %all-gather.23 = f32[1024,128]{1,0:T(8,128)S(1)} all-gather(f32[128,128]{1,0:T(8,128)S(1)} %get-tuple-element.1873), channel_id=25, replica_groups=mesh['row'=8,'col'=4] {'row'}, dimensions={0}, use_global_device_ids=true | all-gather | bytes 589824 | tf_op jit(solution)/shard_map/all_gather | solution.py:17
  557.4 9.3 %while.222 = (s32[]{:T(128)}, f32[384,256]{1,0:T(8,128)S(1)}, s32[]{:T(128)}, f32[4,128,64]{1,2,0:T(8,128)S(1)}, f32[4,64,64]{2,1,0:T(8,128)S(1)}, /*index=5*/s32[]{:T(128)}, s32[]{:T(128)}, s32[]{:T(128)}, s32[]{:T(128)}) while((s32[]{:T(128)}, f32[384,256]{1,0:T(8,128)S(1)}, s32[]{:T(128)}, f32[4,128,64]{1,2,0:T(8,128)S(1)}, ...), condition=%wide.region_25.26_spmd, body=%wide.region_24.25_spmd.sunk | while | flops 62947336 | bytes 1015983 | solution.py:52
  566.6 31.6 %all-gather.26 = f32[1024,128]{1,0:T(8,128)S(1)} all-gather(f32[128,128]{1,0:T(8,128)S(1)} %get-tuple-element.1872), channel_id=28, replica_groups=mesh['row'=8,'col'=4] {'row'}, dimensions={0}, use_global_device_ids=true | all-gather | bytes 589824 | tf_op jit(solution)/shard_map/all_gather | solution.py:17
  598.3 31.4 %all-gather.27 = f32[1024,128]{1,0:T(8,128)S(1)} all-gather(f32[128,128]{1,0:T(8,128)S(1)} %get-tuple-element.1871), channel_id=29, replica_groups=mesh['row'=8,'col'=4] {'row'}, dimensions={0}, use_global_device_ids=true | all-gather | bytes 589824 | tf_op jit(solution)/shard_map/all_gather | solution.py:17
  644.1 9.2 %while.223 = (s32[]{:T(128)}, f32[384,256]{1,0:T(8,128)S(1)}, s32[]{:T(128)}, f32[4,128,64]{1,2,0:T(8,128)S(1)}, f32[4,64,64]{2,1,0:T(8,128)S(1)}, /*index=5*/s32[]{:T(128)}, s32[]{:T(128)}, s32[]{:T(128)}, s32[]{:T(128)}) while((s32[]{:T(128)}, f32[384,256]{1,0:T(8,128)S(1)}, s32[]{:T(128)}, f32[4,128,64]{1,2,0:T(8,128)S(1)}, ...), condition=%wide.region_29.30_spmd, body=%wide.region_28.29_spmd.sunk | while | flops 62947336 | bytes 1015983 | solution.py:52
  653.4 31.8 %all-gather.30 = f32[1024,128]{1,0:T(8,128)S(1)} all-gather(f32[128,128]{1,0:T(8,128)S(1)} %get-tuple-element.1870), channel_id=32, replica_groups=mesh['row'=8,'col'=4] {'row'}, dimensions={0}, use_global_device_ids=true | all-gather | bytes 589824 | tf_op jit(solution)/shard_map/all_gather | solution.py:17
  685.2 31.5 %all-gather.31 = f32[1024,128]{1,0:T(8,128)S(1)} all-gather(f32[128,128]{1,0:T(8,128)S(1)} %get-tuple-element.1869), channel_id=33, replica_groups=mesh['row'=8,'col'=4] {'row'}, dimensions={0}, use_global_device_ids=true | all-gather | bytes 589824 | tf_op jit(solution)/shard_map/all_gather | solution.py:17
  (350 shorter events, 187.3 us)
Async XLA Ops:
  0.0 18.8 %copy-start = (f32[8,1,128,64]{2,3,1,0:T(8,128)S(1)}, f32[8,1,128,64]{2,3,1,0:T(8,128)}, u32[]{:S(2)}) copy-start(f32[8,1,128,64]{2,3,1,0:T(8,128)} %param.38) | copy-start | bytes 786436
  0.9 1.3 copy-start.3
  0.9 32.3 %collective-permute-start = (f32[128,128]{1,0:T(8,128)S(1)}, f32[128,128]{1,0:T(8,128)S(1)}, u32[]{:S(2)}, u32[]{:S(2)}) collective-permute-start(f32[128,128]{1,0:T(8,128)S(1)} %get-tuple-element.1924), channel_id=1, source_target_pairs={{4,0},{8,4},{12,8},{16,12},{20,16},{24,20},{28,24},{5,1},{9,5},{13... | collective-permute-start | bytes 196616 | tf_op jit(solution)/shard_map/ppermute | solution.py:12
  18.8 1.0 copy-start.1
  19.7 0.7 copy-start.2
  110.0 12.1 %collective-permute-start.1 = (f32[128,128]{1,0:T(8,128)S(1)}, f32[128,128]{1,0:T(8,128)S(1)}, u32[]{:S(2)}, u32[]{:S(2)}) collective-permute-start(f32[128,128]{1,0:T(8,128)S(1)} %get-tuple-element.1921), channel_id=1, source_target_pairs={{4,0},{8,4},{12,8},{16,12},{20,16},{24,20},{28,24},{5,1},{9,5},{13... | collective-permute-start | bytes 196616 | tf_op jit(solution)/shard_map/ppermute | solution.py:12
  196.9 12.1 %collective-permute-start.2 = (f32[128,128]{1,0:T(8,128)S(1)}, f32[128,128]{1,0:T(8,128)S(1)}, u32[]{:S(2)}, u32[]{:S(2)}) collective-permute-start(f32[128,128]{1,0:T(8,128)S(1)} %get-tuple-element.1918), channel_id=1, source_target_pairs={{4,0},{8,4},{12,8},{16,12},{20,16},{24,20},{28,24},{5,1},{9,5},{13... | collective-permute-start | bytes 196616 | tf_op jit(solution)/shard_map/ppermute | solution.py:12
  283.8 12.1 %collective-permute-start.3 = (f32[128,128]{1,0:T(8,128)S(1)}, f32[128,128]{1,0:T(8,128)S(1)}, u32[]{:S(2)}, u32[]{:S(2)}) collective-permute-start(f32[128,128]{1,0:T(8,128)S(1)} %get-tuple-element.1915), channel_id=1, source_target_pairs={{4,0},{8,4},{12,8},{16,12},{20,16},{24,20},{28,24},{5,1},{9,5},{13... | collective-permute-start | bytes 196616 | tf_op jit(solution)/shard_map/ppermute | solution.py:12
  371.1 12.1 %collective-permute-start.4 = (f32[128,128]{1,0:T(8,128)S(1)}, f32[128,128]{1,0:T(8,128)S(1)}, u32[]{:S(2)}, u32[]{:S(2)}) collective-permute-start(f32[128,128]{1,0:T(8,128)S(1)} %get-tuple-element.1912), channel_id=1, source_target_pairs={{4,0},{8,4},{12,8},{16,12},{20,16},{24,20},{28,24},{5,1},{9,5},{13... | collective-permute-start | bytes 196616 | tf_op jit(solution)/shard_map/ppermute | solution.py:12
  457.8 12.1 %collective-permute-start.5 = (f32[128,128]{1,0:T(8,128)S(1)}, f32[128,128]{1,0:T(8,128)S(1)}, u32[]{:S(2)}, u32[]{:S(2)}) collective-permute-start(f32[128,128]{1,0:T(8,128)S(1)} %get-tuple-element.1909), channel_id=1, source_target_pairs={{4,0},{8,4},{12,8},{16,12},{20,16},{24,20},{28,24},{5,1},{9,5},{13... | collective-permute-start | bytes 196616 | tf_op jit(solution)/shard_map/ppermute | solution.py:12
  545.0 12.3 %collective-permute-start.6 = (f32[128,128]{1,0:T(8,128)S(1)}, f32[128,128]{1,0:T(8,128)S(1)}, u32[]{:S(2)}, u32[]{:S(2)}) collective-permute-start(f32[128,128]{1,0:T(8,128)S(1)} %get-tuple-element.1906), channel_id=1, source_target_pairs={{4,0},{8,4},{12,8},{16,12},{20,16},{24,20},{28,24},{5,1},{9,5},{13... | collective-permute-start | bytes 196616 | tf_op jit(solution)/shard_map/ppermute | solution.py:12
  632.0 12.1 %collective-permute-start.7 = (f32[128,128]{1,0:T(8,128)S(1)}, f32[128,128]{1,0:T(8,128)S(1)}, u32[]{:S(2)}, u32[]{:S(2)}) collective-permute-start(f32[128,128]{1,0:T(8,128)S(1)} %get-tuple-element.1903), channel_id=1, source_target_pairs={{4,0},{8,4},{12,8},{16,12},{20,16},{24,20},{28,24},{5,1},{9,5},{13... | collective-permute-start | bytes 196616 | tf_op jit(solution)/shard_map/ppermute | solution.py:12
where the time goes:
time: 721 us; the launch traced here: 720 us
  blocking collectives  595 us (83%)
  matrix products  39.6 us (5%)
  local copies, waits for them, and re-layouts  31.9 us (4%)
  loops' own time  24.8 us (3%)
  between operations  16.3 us (2%)
  starting transfers between devices  10.3 us (1%)
    all_gather x16, blocking collectives, entering(): everything = jax.tree.map(lambda part: lax.all_gather(part, axis), array)  507 us
    all_gather x8, blocking collectives, local(): lax.all_gather(own_tri, 'col', axis=0, tiled=True)  44.6 us
    all_gather x8, blocking collectives, local(): lax.all_gather(own_house, 'col', axis=0, tiled=True)  43.4 us
    dynamic_update_slice x32, local copies, waits for them, and re-layouts, advance(): lax.dynamic_update_slice_in_dim(current, reflect(segment, householder, tr...  28.6 us
    another operation x8, loops' own time, sweep_apply(): return lax.fori_loop(0, house_set.shape[0], advance, extended)  22.6 us
  transfers between devices with their start and end apart: 8, of which 0 were waited for; matrix products, arithmetic and copies ran while one was open for 0% of the time, Pallas kernels for 0%

commit v1 on v0

--- a/solution.py
+++ b/solution.py
@@ -4,6 +4,27 @@
 from jax.sharding import PartitionSpec as P
 
 highest = lax.Precision.HIGHEST
+
+
+def ring_gather(shard, axis, dim):
+    size, position, span = (lax.axis_size(axis), lax.axis_index(axis), shard.shape[dim])
+    upward = [(i, (i + 1) % size) for i in range(size)]
+    left = [(i, (i - 1) % size) for i in range(size)]
+    whole = jnp.zeros((*shard.shape[:dim], size * span, *shard.shape[dim + 1 :]), shard.dtype)
+    whole = lax.dynamic_update_slice_in_dim(whole, shard, position * span, axis=dim)
+    from_left = from_right = shard
+    halfway = size // 2
+    for step in range(1, halfway + 1):
+        from_left = lax.ppermute(from_left, axis, upward)
+        whole = lax.dynamic_update_slice_in_dim(
+            whole, from_left, (position - step) % size * span, axis=dim
+        )
+        if step < size - halfway:
+            from_right = lax.ppermute(from_right, axis, left)
+            whole = lax.dynamic_update_slice_in_dim(
+                whole, from_right, (position + step) % size * span, axis=dim
+            )
+    return whole
 
 
 def passed_along(block, axis, distance):
@@ -76,7 +97,7 @@
         own_house = lax.dynamic_index_in_dim(reflectors, stored, 0, keepdims=False)
         own_tri = lax.dynamic_index_in_dim(factors, stored, 0, keepdims=False)
         house_set, tri_set = (
-            lax.all_gather(own_house, "col", axis=0, tiled=True),
+            ring_gather(own_house, "col", 0),
             lax.all_gather(own_tri, "col", axis=0, tiled=True),
         )
         next_rows = passed_along(vectors[:span_rows], "row", -1)

time: 721 us -> 793 us (1.100)
  matrix products: 39.6 us -> 81.1 us
  blocking collectives: 595 us -> 560 us
  waiting for transfers between devices: 0.02 us -> 29.1 us
  starting transfers between devices: 10.3 us -> 28.8 us
  local copies, waits for them, and re-layouts: 31.9 us -> 49.7 us
    all_gather x8 -> x0, blocking collectives: 43.4 us -> none  [local(): lax.all_gather(own_house, 'col', axis=0, tiled=True)]
    ppermute x8, waiting for transfers between devices: 0.02 us -> 29 us  [passed_along(): return lax.ppermute(block, axis, route)]
    dot_general x32, matrix products: 6.26 us -> 27.5 us  [reflect(): jnp.dot(triangle, inner, precision=highest, preferred_element_type=jnp.fl...]
    dot_general x64, matrix products: 13.4 us -> 33.9 us  [compose(): jnp.dot(later[0], earlier[1], precision=highest, preferred_element_type=j...]
    ppermute x0 -> x24, starting transfers between devices: none -> 18.3 us  [the longest x8 13.3 us: ring_gather(): from_right = lax.ppermute(from_right, axis, left)]
    dynamic_update_slice x0 -> x32, local copies, waits for them, and re-layouts: none -> 14.6 us  [the longest x16 12.7 us: ring_gather(): lax.dynamic_update_slice_in_dim(whole, from_left, (position - step) % siz...]
  transfers between devices with their start and end apart: 8 -> 32, of which waited for: 0 -> 8; matrix products, arithmetic and copies ran while one was open for 0% -> 15% of each run, Pallas kernels for 0% -> 0%
where the time goes in v1:
time: 793 us; the launch traced here: 789 us
  blocking collectives  560 us (71%)
  matrix products  81.1 us (10%)
  local copies, waits for them, and re-layouts  49.7 us (6%)
  waiting for transfers between devices  29.1 us (4%)
  starting transfers between devices  28.8 us (4%)
  loops' own time  23.3 us (3%)
  between operations  16 us (2%)
    all_gather x16, blocking collectives, entering(): everything = jax.tree.map(lambda part: lax.all_gather(part, axis), array)  512 us
    all_gather x8, blocking collectives, local(): lax.all_gather(own_tri, 'col', axis=0, tiled=True)  47.1 us
    dot_general x64, matrix products, compose(): jnp.dot(later[0], earlier[1], precision=highest, preferred_element_type=j...  33.9 us
    ppermute x8, waiting for transfers between devices, passed_along(): return lax.ppermute(block, axis, route)  29 us
    dynamic_update_slice x32, local copies, waits for them, and re-layouts, advance(): lax.dynamic_update_slice_in_dim(current, reflect(segment, householder, tr...  28.6 us
    dot_general x32, matrix products, reflect(): jnp.dot(triangle, inner, precision=highest, preferred_element_type=jnp.fl...  27.5 us
    another operation x8, loops' own time, sweep_apply(): return lax.fori_loop(0, house_set.shape[0], advance, extended)  21.1 us
  transfers between devices with their start and end apart: 32, of which 8 were waited for; matrix products, arithmetic and copies ran while one was open for 15% of the time, Pallas kernels for 0%

profile of v1, /device:TPU:0, one launch (start us, length us, event | category | flops | bytes accessed | tf_op | source)
XLA Modules:
  0.0 788.6 jit_solution(1463450017836296087)
XLA Ops:
  98.2 12.0 %while.216 = (s32[]{:T(128)}, f32[384,256]{1,0:T(8,128)S(1)}, s32[]{:T(128)}, f32[4,128,64]{2,1,0:T(8,128)S(1)}, f32[4,64,64]{2,1,0:T(8,128)}, /*index=5*/s32[]{:T(128)}, s32[]{:T(128)}, s32[]{:T(128)}, s32[]{:T(128)}) while((s32[]{:T(128)}, f32[384,256]{1,0:T(8,128)S(1)}, s32[]{:T(128)}, f32[4,128,64]{2,1,0:T(8,128)S(1)}, ...), condition=%wide.region_1.2_spmd, body=%wide.region_0.1_spmd.sunk | while | flops 62947336 | bytes 1082027 | solution.py:73
  110.2 35.9 %all-gather.1 = f32[1024,128]{1,0:T(8,128)} all-gather(f32[128,128]{1,0:T(8,128)S(1)} %get-tuple-element.1844), channel_id=3, replica_groups=mesh['row'=8,'col'=4] {'row'}, dimensions={0}, use_global_device_ids=true | all-gather | bytes 589824 | tf_op jit(solution)/shard_map/all_gather | solution.py:38
  146.1 33.5 %all-gather.2 = f32[1024,128]{1,0:T(8,128)} all-gather(f32[128,128]{1,0:T(8,128)S(1)} %get-tuple-element.1843), channel_id=4, replica_groups=mesh['row'=8,'col'=4] {'row'}, dimensions={0}, use_global_device_ids=true | all-gather | bytes 589824 | tf_op jit(solution)/shard_map/all_gather | solution.py:38
  179.6 9.0 %while.224 = (s32[]{:T(128)}, f32[128,128]{1,0:T(8,128)S(1)}, s32[]{:T(128)}, f32[8,128,128]{2,1,0:T(8,128)}, f32[8,128,128]{2,1,0:T(8,128)}, /*index=5*/s32[]{:T(128)}, s32[]{:T(128)}) while((s32[]{:T(128)}, f32[128,128]{1,0:T(8,128)S(1)}, s32[]{:T(128)}, f32[8,128,128]{2,1,0:T(8,128)}, f32[8,128,128]{2,1,0:T(8,128)}, ...), condition=%wide.region_3.4_spmd.clone, body=%wide.region_2.3_spmd.clone.sunk | while | flops 25231364 | bytes 461407 | solution.py:50
  195.1 11.9 %while.217 = (s32[]{:T(128)}, f32[384,256]{1,0:T(8,128)S(1)}, s32[]{:T(128)}, f32[4,128,64]{2,1,0:T(8,128)S(1)}, f32[4,64,64]{2,1,0:T(8,128)}, /*index=5*/s32[]{:T(128)}, s32[]{:T(128)}, s32[]{:T(128)}, s32[]{:T(128)}) while((s32[]{:T(128)}, f32[384,256]{1,0:T(8,128)S(1)}, s32[]{:T(128)}, f32[4,128,64]{2,1,0:T(8,128)S(1)}, ...), condition=%wide.region_5.6_spmd, body=%wide.region_4.5_spmd.sunk | while | flops 62947336 | bytes 1082027 | solution.py:73
  207.0 31.7 %all-gather.4 = f32[1024,128]{1,0:T(8,128)S(1)} all-gather(f32[128,128]{1,0:T(8,128)S(1)} %get-tuple-element.1842), channel_id=6, replica_groups=mesh['row'=8,'col'=4] {'row'}, dimensions={0}, use_global_device_ids=true | all-gather | bytes 589824 | tf_op jit(solution)/shard_map/all_gather | solution.py:38
  238.7 33.5 %all-gather.5 = f32[1024,128]{1,0:T(8,128)} all-gather(f32[128,128]{1,0:T(8,128)S(1)} %get-tuple-element.1841), channel_id=7, replica_groups=mesh['row'=8,'col'=4] {'row'}, dimensions={0}, use_global_device_ids=true | all-gather | bytes 589824 | tf_op jit(solution)/shard_map/all_gather | solution.py:38
  287.5 12.1 %while.218 = (s32[]{:T(128)}, f32[384,256]{1,0:T(8,128)S(1)}, s32[]{:T(128)}, f32[4,128,64]{2,1,0:T(8,128)S(1)}, f32[4,64,64]{2,1,0:T(8,128)}, /*index=5*/s32[]{:T(128)}, s32[]{:T(128)}, s32[]{:T(128)}, s32[]{:T(128)}) while((s32[]{:T(128)}, f32[384,256]{1,0:T(8,128)S(1)}, s32[]{:T(128)}, f32[4,128,64]{2,1,0:T(8,128)S(1)}, ...), condition=%wide.region_9.10_spmd, body=%wide.region_8.9_spmd.sunk | while | flops 62947336 | bytes 1082027 | solution.py:73
  299.6 31.5 %all-gather.7 = f32[1024,128]{1,0:T(8,128)S(1)} all-gather(f32[128,128]{1,0:T(8,128)S(1)} %get-tuple-element.1840), channel_id=9, replica_groups=mesh['row'=8,'col'=4] {'row'}, dimensions={0}, use_global_device_ids=true | all-gather | bytes 589824 | tf_op jit(solution)/shard_map/all_gather | solution.py:38
  331.1 33.4 %all-gather.8 = f32[1024,128]{1,0:T(8,128)} all-gather(f32[128,128]{1,0:T(8,128)S(1)} %get-tuple-element.1839), channel_id=10, replica_groups=mesh['row'=8,'col'=4] {'row'}, dimensions={0}, use_global_device_ids=true | all-gather | bytes 589824 | tf_op jit(solution)/shard_map/all_gather | solution.py:38
  379.7 12.3 %while.219 = (s32[]{:T(128)}, f32[384,256]{1,0:T(8,128)S(1)}, s32[]{:T(128)}, f32[4,128,64]{2,1,0:T(8,128)S(1)}, f32[4,64,64]{2,1,0:T(8,128)}, /*index=5*/s32[]{:T(128)}, s32[]{:T(128)}, s32[]{:T(128)}, s32[]{:T(128)}) while((s32[]{:T(128)}, f32[384,256]{1,0:T(8,128)S(1)}, s32[]{:T(128)}, f32[4,128,64]{2,1,0:T(8,128)S(1)}, ...), condition=%wide.region_13.14_spmd, body=%wide.region_12.13_spmd.sunk | while | flops 62947336 | bytes 1082027 | solution.py:73
  392.1 31.5 %all-gather.10 = f32[1024,128]{1,0:T(8,128)S(1)} all-gather(f32[128,128]{1,0:T(8,128)S(1)} %get-tuple-element.1838), channel_id=12, replica_groups=mesh['row'=8,'col'=4] {'row'}, dimensions={0}, use_global_device_ids=true | all-gather | bytes 589824 | tf_op jit(solution)/shard_map/all_gather | solution.py:38
  423.6 31.3 %all-gather.11 = f32[1024,128]{1,0:T(8,128)S(1)} all-gather(f32[128,128]{1,0:T(8,128)S(1)} %get-tuple-element.1837), channel_id=13, replica_groups=mesh['row'=8,'col'=4] {'row'}, dimensions={0}, use_global_device_ids=true | all-gather | bytes 589824 | tf_op jit(solution)/shard_map/all_gather | solution.py:38
  463.7 12.4 %while.220 = (s32[]{:T(128)}, f32[384,256]{1,0:T(8,128)S(1)}, s32[]{:T(128)}, f32[4,128,64]{2,1,0:T(8,128)S(1)}, f32[4,64,64]{2,1,0:T(8,128)}, /*index=5*/s32[]{:T(128)}, s32[]{:T(128)}, s32[]{:T(128)}, s32[]{:T(128)}) while((s32[]{:T(128)}, f32[384,256]{1,0:T(8,128)S(1)}, s32[]{:T(128)}, f32[4,128,64]{2,1,0:T(8,128)S(1)}, ...), condition=%wide.region_17.18_spmd, body=%wide.region_16.17_spmd.sunk | while | flops 62947336 | bytes 1082027 | solution.py:73
  476.1 31.5 %all-gather.13 = f32[1024,128]{1,0:T(8,128)S(1)} all-gather(f32[128,128]{1,0:T(8,128)S(1)} %get-tuple-element.1836), channel_id=15, replica_groups=mesh['row'=8,'col'=4] {'row'}, dimensions={0}, use_global_device_ids=true | all-gather | bytes 589824 | tf_op jit(solution)/shard_map/all_gather | solution.py:38
  507.6 31.2 %all-gather.14 = f32[1024,128]{1,0:T(8,128)S(1)} all-gather(f32[128,128]{1,0:T(8,128)S(1)} %get-tuple-element.1835), channel_id=16, replica_groups=mesh['row'=8,'col'=4] {'row'}, dimensions={0}, use_global_device_ids=true | all-gather | bytes 589824 | tf_op jit(solution)/shard_map/all_gather | solution.py:38
  547.5 12.4 %while.221 = (s32[]{:T(128)}, f32[384,256]{1,0:T(8,128)S(1)}, s32[]{:T(128)}, f32[4,128,64]{2,1,0:T(8,128)S(1)}, f32[4,64,64]{2,1,0:T(8,128)}, /*index=5*/s32[]{:T(128)}, s32[]{:T(128)}, s32[]{:T(128)}, s32[]{:T(128)}) while((s32[]{:T(128)}, f32[384,256]{1,0:T(8,128)S(1)}, s32[]{:T(128)}, f32[4,128,64]{2,1,0:T(8,128)S(1)}, ...), condition=%wide.region_21.22_spmd, body=%wide.region_20.21_spmd.sunk | while | flops 62947336 | bytes 1082027 | solution.py:73
  559.9 31.2 %all-gather.16 = f32[1024,128]{1,0:T(8,128)S(1)} all-gather(f32[128,128]{1,0:T(8,128)S(1)} %get-tuple-element.1834), channel_id=18, replica_groups=mesh['row'=8,'col'=4] {'row'}, dimensions={0}, use_global_device_ids=true | all-gather | bytes 589824 | tf_op jit(solution)/shard_map/all_gather | solution.py:38
  591.1 31.5 %all-gather.17 = f32[1024,128]{1,0:T(8,128)S(1)} all-gather(f32[128,128]{1,0:T(8,128)S(1)} %get-tuple-element.1833), channel_id=19, replica_groups=mesh['row'=8,'col'=4] {'row'}, dimensions={0}, use_global_device_ids=true | all-gather | bytes 589824 | tf_op jit(solution)/shard_map/all_gather | solution.py:38
  631.2 12.3 %while.222 = (s32[]{:T(128)}, f32[384,256]{1,0:T(8,128)S(1)}, s32[]{:T(128)}, f32[4,128,64]{2,1,0:T(8,128)S(1)}, f32[4,64,64]{2,1,0:T(8,128)}, /*index=5*/s32[]{:T(128)}, s32[]{:T(128)}, s32[]{:T(128)}, s32[]{:T(128)}) while((s32[]{:T(128)}, f32[384,256]{1,0:T(8,128)S(1)}, s32[]{:T(128)}, f32[4,128,64]{2,1,0:T(8,128)S(1)}, ...), condition=%wide.region_25.26_spmd, body=%wide.region_24.25_spmd.sunk | while | flops 62947336 | bytes 1082027 | solution.py:73
  643.5 31.2 %all-gather.19 = f32[1024,128]{1,0:T(8,128)S(1)} all-gather(f32[128,128]{1,0:T(8,128)S(1)} %get-tuple-element.1832), channel_id=21, replica_groups=mesh['row'=8,'col'=4] {'row'}, dimensions={0}, use_global_device_ids=true | all-gather | bytes 589824 | tf_op jit(solution)/shard_map/all_gather | solution.py:38
  674.7 31.2 %all-gather.20 = f32[1024,128]{1,0:T(8,128)S(1)} all-gather(f32[128,128]{1,0:T(8,128)S(1)} %get-tuple-element.1831), channel_id=22, replica_groups=mesh['row'=8,'col'=4] {'row'}, dimensions={0}, use_global_device_ids=true | all-gather | bytes 589824 | tf_op jit(solution)/shard_map/all_gather | solution.py:38
  723.3 31.2 %all-gather.22 = f32[1024,128]{1,0:T(8,128)S(1)} all-gather(f32[128,128]{1,0:T(8,128)S(1)} %get-tuple-element.1830), channel_id=24, replica_groups=mesh['row'=8,'col'=4] {'row'}, dimensions={0}, use_global_device_ids=true | all-gather | bytes 589824 | tf_op jit(solution)/shard_map/all_gather | solution.py:38
  754.5 31.2 %all-gather.23 = f32[1024,128]{1,0:T(8,128)S(1)} all-gather(f32[128,128]{1,0:T(8,128)S(1)} %get-tuple-element.1829), channel_id=25, replica_groups=mesh['row'=8,'col'=4] {'row'}, dimensions={0}, use_global_device_ids=true | all-gather | bytes 589824 | tf_op jit(solution)/shard_map/all_gather | solution.py:38
  (442 shorter events, 273.2 us)
Async XLA Ops:
  17.7 56.6 %collective-permute-start.1 = (f32[1,128,64]{2,1,0:T(8,128)S(1)}, f32[1,128,64]{2,1,0:T(8,128)}, u32[]{:S(2)}, u32[]{:S(2)}) collective-permute-start(f32[1,128,64]{2,1,0:T(8,128)S(1)} %bitcast.329), channel_id=1, source_target_pairs={{0,1},{1,2},{2,3},{3,0},{4,5},{5,6},{6,7},{7,4},{8,9},{9,10},{10,1... | collective-permute-start | bytes 98312 | tf_op jit(solution)/shard_map/ppermute | solution.py:18
  18.3 59.1 %collective-permute-start.2 = (f32[1,128,64]{2,1,0:T(8,128)S(1)}, f32[1,128,64]{2,1,0:T(8,128)}, u32[]{:S(2)}, u32[]{:S(2)}) collective-permute-start(f32[1,128,64]{2,1,0:T(8,128)S(1)} %bitcast.330), channel_id=1, source_target_pairs={{0,3},{1,0},{2,1},{3,2},{4,7},{5,4},{6,5},{7,6},{8,11},{9,8},{10,9... | collective-permute-start | bytes 98312 | tf_op jit(solution)/shard_map/ppermute | solution.py:23
  20.4 56.0 %collective-permute-start.5 = (f32[1,128,64]{2,1,0:T(8,128)S(1)}, f32[1,128,64]{2,1,0:T(8,128)}, u32[]{:S(2)}, u32[]{:S(2)}) collective-permute-start(f32[1,128,64]{2,1,0:T(8,128)S(1)} %bitcast.327), channel_id=1, source_target_pairs={{0,1},{1,2},{2,3},{3,0},{4,5},{5,6},{6,7},{7,4},{8,9},{9,10},{10,1... | collective-permute-start | bytes 98312 | tf_op jit(solution)/shard_map/ppermute | solution.py:18
  21.0 58.9 %collective-permute-start.6 = (f32[1,128,64]{2,1,0:T(8,128)S(1)}, f32[1,128,64]{2,1,0:T(8,128)}, u32[]{:S(2)}, u32[]{:S(2)}) collective-permute-start(f32[1,128,64]{2,1,0:T(8,128)S(1)} %bitcast.328), channel_id=1, source_target_pairs={{0,3},{1,0},{2,1},{3,2},{4,7},{5,4},{6,5},{7,6},{8,11},{9,8},{10,9... | collective-permute-start | bytes 98312 | tf_op jit(solution)/shard_map/ppermute | solution.py:23
  22.3 58.6 %collective-permute-start.9 = (f32[1,128,64]{2,1,0:T(8,128)S(1)}, f32[1,128,64]{2,1,0:T(8,128)}, u32[]{:S(2)}, u32[]{:S(2)}) collective-permute-start(f32[1,128,64]{2,1,0:T(8,128)S(1)} %bitcast.323), channel_id=1, source_target_pairs={{0,1},{1,2},{2,3},{3,0},{4,5},{5,6},{6,7},{7,4},{8,9},{9,10},{10,1... | collective-permute-start | bytes 98312 | tf_op jit(solution)/shard_map/ppermute | solution.py:18
  74.3 9.2 %collective-permute-start.10 = (f32[1,128,64]{2,1,0:T(8,128)S(1)}, f32[1,128,64]{2,1,0:T(8,128)S(1)}, u32[]{:S(2)}, u32[]{:S(2)}) collective-permute-start(f32[1,128,64]{2,1,0:T(8,128)S(1)} %bitcast.324), channel_id=1, source_target_pairs={{0,3},{1,0},{2,1},{3,2},{4,7},{5,4},{6,5},{7,6},{8,11},{9,8},{10,9... | collective-permute-start | bytes 98312 | tf_op jit(solution)/shard_map/ppermute | solution.py:23
  76.4 7.2 collective-permute-start.13
  77.4 8.9 %collective-permute-start.14 = (f32[1,128,64]{2,1,0:T(8,128)S(1)}, f32[1,128,64]{2,1,0:T(8,128)S(1)}, u32[]{:S(2)}, u32[]{:S(2)}) collective-permute-start(f32[1,128,64]{2,1,0:T(8,128)S(1)} %bitcast.334), channel_id=1, source_target_pairs={{0,3},{1,0},{2,1},{3,2},{4,7},{5,4},{6,5},{7,6},{8,11},{9,8},{10,9... | collective-permute-start | bytes 98312 | tf_op jit(solution)/shard_map/ppermute | solution.py:23
  80.0 6.3 collective-permute-start.17
  80.9 8.1 %collective-permute-start.18 = (f32[1,128,64]{2,1,0:T(8,128)S(1)}, f32[1,128,64]{2,1,0:T(8,128)S(1)}, u32[]{:S(2)}, u32[]{:S(2)}) collective-permute-start(f32[1,128,64]{2,1,0:T(8,128)S(1)} %bitcast.332), channel_id=1, source_target_pairs={{0,3},{1,0},{2,1},{3,2},{4,7},{5,4},{6,5},{7,6},{8,11},{9,8},{10,9... | collective-permute-start | bytes 98312 | tf_op jit(solution)/shard_map/ppermute | solution.py:23
  83.6 8.1 %collective-permute-start.22 = (f32[1,128,64]{2,1,0:T(8,128)S(1)}, f32[1,128,64]{2,1,0:T(8,128)S(1)}, u32[]{:S(2)}, u32[]{:S(2)}) collective-permute-start(f32[1,128,64]{2,1,0:T(8,128)S(1)} %bitcast.326), channel_id=1, source_target_pairs={{0,3},{1,0},{2,1},{3,2},{4,7},{5,4},{6,5},{7,6},{8,11},{9,8},{10,9... | collective-permute-start | bytes 98312 | tf_op jit(solution)/shard_map/ppermute | solution.py:23
  86.2 6.8 collective-permute-start.25
  86.3 7.6 collective-permute-start.26
  89.0 6.7 collective-permute-start.30
  93.9 94.9 %collective-permute-start.7 = (f32[1,128,64]{2,1,0:T(8,128)}, f32[1,128,64]{2,1,0:T(8,128)}, u32[]{:S(2)}, u32[]{:S(2)}) collective-permute-start(f32[1,128,64]{2,1,0:T(8,128)} %collective-permute-done.5), channel_id=1, source_target_pairs={{0,1},{1,2},{2,3},{3,0},{4,5},{5,6},{6,7},{7,4},{8,9},{9,10},{10,1... | collective-permute-start | bytes 98312 | tf_op jit(solution)/shard_map/ppermute | solution.py:18
  94.8 186.5 %collective-permute-start.11 = (f32[1,128,64]{2,1,0:T(8,128)}, f32[1,128,64]{2,1,0:T(8,128)}, u32[]{:S(2)}, u32[]{:S(2)}) collective-permute-start(f32[1,128,64]{2,1,0:T(8,128)} %collective-permute-done.9), channel_id=1, source_target_pairs={{0,1},{1,2},{2,3},{3,0},{4,5},{5,6},{6,7},{7,4},{8,9},{9,10},{10,1... | collective-permute-start | bytes 98312 | tf_op jit(solution)/shard_map/ppermute | solution.py:18
  95.7 277.8 %collective-permute-start.15 = (f32[1,128,64]{2,1,0:T(8,128)}, f32[1,128,64]{2,1,0:T(8,128)}, u32[]{:S(2)}, u32[]{:S(2)}) collective-permute-start(f32[1,128,64]{2,1,0:T(8,128)} %collective-permute-done.13), channel_id=1, source_target_pairs={{0,1},{1,2},{2,3},{3,0},{4,5},{5,6},{6,7},{7,4},{8,9},{9,10},{10,1... | collective-permute-start | bytes 98312 | tf_op jit(solution)/shard_map/ppermute | solution.py:18
  97.2 361.4 %collective-permute-start.19 = (f32[1,128,64]{2,1,0:T(8,128)}, f32[1,128,64]{2,1,0:T(8,128)}, u32[]{:S(2)}, u32[]{:S(2)}) collective-permute-start(f32[1,128,64]{2,1,0:T(8,128)} %collective-permute-done.17), channel_id=1, source_target_pairs={{0,1},{1,2},{2,3},{3,0},{4,5},{5,6},{6,7},{7,4},{8,9},{9,10},{10,1... | collective-permute-start | bytes 98312 | tf_op jit(solution)/shard_map/ppermute | solution.py:18
  97.8 444.6 %collective-permute-start.23 = (f32[1,128,64]{2,1,0:T(8,128)}, f32[1,128,64]{2,1,0:T(8,128)}, u32[]{:S(2)}, u32[]{:S(2)}) collective-permute-start(f32[1,128,64]{2,1,0:T(8,128)} %collective-permute-done.21), channel_id=1, source_target_pairs={{0,1},{1,2},{2,3},{3,0},{4,5},{5,6},{6,7},{7,4},{8,9},{9,10},{10,1... | collective-permute-start | bytes 98312 | tf_op jit(solution)/shard_map/ppermute | solution.py:18
  195.0 431.2 %collective-permute-start.27 = (f32[1,128,64]{2,1,0:T(8,128)}, f32[1,128,64]{2,1,0:T(8,128)}, u32[]{:S(2)}, u32[]{:S(2)}) collective-permute-start(f32[1,128,64]{2,1,0:T(8,128)} %collective-permute-done.25), channel_id=1, source_target_pairs={{0,1},{1,2},{2,3},{3,0},{4,5},{5,6},{6,7},{7,4},{8,9},{9,10},{10,1... | collective-permute-start | bytes 98312 | tf_op jit(solution)/shard_map/ppermute | solution.py:18
  287.4 422.1 %collective-permute-start.31 = (f32[1,128,64]{2,1,0:T(8,128)}, f32[1,128,64]{2,1,0:T(8,128)}, u32[]{:S(2)}, u32[]{:S(2)}) collective-permute-start(f32[1,128,64]{2,1,0:T(8,128)} %collective-permute-done.29), channel_id=1, source_target_pairs={{0,1},{1,2},{2,3},{3,0},{4,5},{5,6},{6,7},{7,4},{8,9},{9,10},{10,1... | collective-permute-start | bytes 98312 | tf_op jit(solution)/shard_map/ppermute | solution.py:18
  457.1 6.5 collective-permute-start.16
  541.1 6.4 collective-permute-start.20
  624.9 6.2 collective-permute-start.24
  (14 other events, 77.5 us)
